TPU v7x, 128 devices: a whole 4x4x4 slice. The times are simulated.
128 devices in a mesh: replica: 1, dp: 128 (over z, y, x, core).
Axes of the slice: x: 4, y: 4, z: 4, core: 2. Of those that a mesh axis runs over, the one named last changes fastest.
Arguments:
- x: bfloat16 [256, 2048], P(('replica', 'dp'))
- lengths: int32 [256], P(('replica', 'dp'))
- cache: bfloat16 [2, 256, 1024, 576], P(None, ('replica', 'dp'))
- attn_gain: float32 [2, 2048], replicated
- ffn_gain: float32 [2, 2048], replicated
- w_query: bfloat16 [2, 2048, 9216], replicated
- w_attn_out: bfloat16 [2, 8192, 2048], replicated
- w_up: bfloat16 [2, 2048, 11264], P(None, None, 'dp')
- w_gate: bfloat16 [2, 2048, 11264], P(None, None, 'dp')
- w_down: bfloat16 [2, 11264, 2048], P(None, 'dp')
Outputs:
- output: bfloat16 [256, 2048], P(('replica', 'dp'))
All inputs are finite; a program needn't handle non-finite values.
Results may differ from a plain program's by a relative error of at most 0.02.
Values are sent between devices in bfloat16 or wider.
A program may use at most 1 GiB of HBM per device.

v0:
```python
import jax
import jax.numpy as jnp
from jax import lax
from jax.sharding import PartitionSpec as P

NORM_EPS = 1e-6


def rms_norm(rows, gain):
    rows_f = rows.astype(jnp.float32)
    mean_sq = jnp.mean(rows_f * rows_f, axis=-1, keepdims=True)
    return (rows_f * lax.rsqrt(mean_sq + NORM_EPS) * gain).astype(jnp.bfloat16)


def local_attention(x_rows, len_rows, cache_l, gain, wq_l, wo_l):
    rows, seq_len, kv_dim = cache_l.shape
    heads = wq_l.shape[1] // kv_dim
    latent = wo_l.shape[0] // heads
    d_model = wo_l.shape[1]
    scale = (3 * (kv_dim - latent)) ** -0.5
    normed = rms_norm(x_rows, gain)
    query = jnp.dot(normed, wq_l, preferred_element_type=jnp.float32).astype(jnp.bfloat16)
    query = query.reshape(rows, heads, kv_dim)
    scores = jnp.einsum('bhc,btc->bht', query, cache_l, preferred_element_type=jnp.float32) * scale
    positions = lax.broadcasted_iota(jnp.int32, (1, 1, seq_len), 2)
    scores = jnp.where(positions < len_rows[:, None, None], scores, -jnp.inf)
    attn_probs = jax.nn.softmax(scores, axis=-1).astype(jnp.bfloat16)
    mixed = jnp.einsum('bht,btc->bhc', attn_probs, cache_l, preferred_element_type=jnp.float32)
    mixed = mixed[:, :, :latent].astype(jnp.bfloat16)
    attn_out = jnp.einsum('bhc,hcd->bd', mixed, wo_l.reshape(heads, latent, d_model), preferred_element_type=jnp.float32)
    return (x_rows.astype(jnp.float32) + attn_out).astype(jnp.bfloat16)


def solution(mesh):
    row_axes = ('replica', 'dp')

    def local_step(x_rows, len_rows, cache, attn_gain, ffn_gain, w_query, w_attn_out, w_up, w_gate, w_down):
        for layer_idx in range(cache.shape[0]):
            x_rows = local_attention(x_rows, len_rows, cache[layer_idx], attn_gain[layer_idx], w_query[layer_idx], w_attn_out[layer_idx])
            normed = rms_norm(x_rows, ffn_gain[layer_idx])
            gathered = lax.all_gather(normed, 'dp', axis=0, tiled=True)
            gate_pre = jnp.dot(gathered, w_gate[layer_idx], preferred_element_type=jnp.float32)
            up_pre = jnp.dot(gathered, w_up[layer_idx], preferred_element_type=jnp.float32)
            hidden = (jax.nn.silu(gate_pre) * up_pre).astype(jnp.bfloat16)
            partial_out = jnp.dot(hidden, w_down[layer_idx], preferred_element_type=jnp.float32)
            ffn_rows = lax.psum_scatter(partial_out, 'dp', scatter_dimension=0, tiled=True)
            x_rows = (x_rows.astype(jnp.float32) + ffn_rows).astype(jnp.bfloat16)
        return x_rows

    return jax.shard_map(
        local_step,
        mesh=mesh,
        in_specs=(P(row_axes, None), P(row_axes), P(None, row_axes, None, None), P(), P(), P(), P(),
                  P(None, None, 'dp'), P(None, None, 'dp'), P(None, 'dp', None)),
        out_specs=P(row_axes, None),
        check_vma=False,
    )
```

profile of v0, /device:TPU:0, one launch (start us, length us, event | category | flops | bytes accessed | tf_op | source)
XLA Modules:
  0.0 563.9 jit_solution(5748970658202352341)
XLA Ops:
  6.5 0.0 all-gather.5.cloned.1.call-start
  6.5 0.8 fusion.105
  7.3 0.8 fusion.84
  8.2 0.0 copy-start.5
  8.2 14.3 %fusion.8 = bf16[2,9216]{1,0:T(2,128)(2,1)S(1)} fusion(bf16[2,2048,9216]{2,1,0:T(8,128)(2,1)} %param.15, bf16[2,2048]{1,0:T(2,128)(2,1)} %param.10, f32[2]{0:T(128)S(1)} %add_rsqrt_fusion.3, f32[2048]{0:T(1024)S(1)} %bitcast.89), kind=kOutput, calls=%fused_computation.8 | convolution fusion | flops 75532288 | bytes 37801992 | tf_op jit(solution)/shard_map/dot_general | solution.py:22
  22.5 0.1 reshape.63
  22.7 0.0 copy-done.5
  22.7 0.1 iota_compare_fusion
  22.7 2.1 fusion.37
  24.9 0.2 fusion.106
  25.0 2.4 fusion.18
  27.4 0.0 copy-start.3
  27.5 43.5 %fusion.103 = (bf16[1,8192,2048]{2,1,0:T(8,128)(2,1)}, bf16[1,8192,2048]{2,1,0:T(8,128)(2,1)}) fusion(bf16[2,8192,2048]{2,1,0:T(8,128)(2,1)} %param.16), kind=kLoop, calls=%fused_computation.107 | loop fusion | bytes 134217728 | tf_op jit(solution)/shard_map/slice | solution.py:39
  71.0 0.0 copy-done.3
  71.0 0.0 copy-start.4
  71.0 0.0 copy-start
  71.0 0.0 copy-start.1
  71.0 0.0 copy-start.2
  71.0 13.1 %multiply_reduce_fusion.1 = (f32[2]{0:T(128)S(1)}, f32[2,2048]{1,0:T(2,128)S(1)}) fusion(bf16[16,512,2048]{2,1,0:T(8,128)(2,1)} %bitcast.87, bf16[2,16,512]{2,1,0:T(8,128)(2,1)S(1)} %slice.74, bf16[2,2048]{1,0:T(2,128)(2,1)S(1)} %copy-done.3), kind=kOutput, calls=%fused_computation.93 | convolution fusion | flops 67133440 | bytes 33611784 | tf_op jit(solution)/shard_map/bhc,hcd->bd/dot_general | solution.py:30
  84.2 0.0 copy-done.4
  84.2 0.7 fusion.96
  84.9 0.0 all-gather.5.cloned.1.call-update
  84.9 0.0 all-reduce.5.cloned.1.call-start
  84.9 66.2 %all-gather.5.cloned.1.call-done = bf16[128,2,2048]{2,1,0:T(2,128)(2,1)} async-done(((bf16[1,2,2048]{2,1,0:T(2,128)(2,1)}), bf16[128,2,2048]{2,1,0:T(2,128)(2,1)}) %all-gather.5.cloned.1.call-update) | async-done | bytes 1048592 | tf_op jit(solution)/shard_map/all_gather | solution.py:41
  151.2 1.5 reshape.66
  152.6 0.0 copy-done
  152.7 0.5 fusion.60
  153.1 0.0 copy-done.1
  153.1 0.0 copy-done.2
  153.1 2.8 fusion.51
  155.9 0.0 all-reduce.5.cloned.1.call-update
  155.9 0.2 all-gather.7.cloned.1.call-start
  156.2 149.5 %all-reduce.5.cloned.1.call-done = f32[256,2048]{1,0:T(8,128)} async-done(((f32[256,2048]{1,0:T(8,128)}), f32[256,2048]{1,0:T(8,128)}) %all-reduce.5.cloned.1.call-update) | async-done | bytes 2097168
  305.7 1.0 fusion.87
  306.7 14.4 %fusion.11 = bf16[2,9216]{1,0:T(2,128)(2,1)S(1)} fusion(bf16[2,2048,9216]{2,1,0:T(8,128)(2,1)} %param.15, bf16[2,2048]{1,0:T(2,128)(2,1)S(1)} %get-tuple-element.6, f32[2]{0:T(128)S(1)} %add_rsqrt_fusion.1, f32[2048]{0:T(1024)S(1)} %bitcast.88), kind=kOutput, calls=%fused_computation.9 | convolution fusion | flops 75532288 | bytes 37801992 | tf_op jit(solution)/shard_map/dot_general | solution.py:22
  321.0 0.1 reshape.64
  321.2 2.1 fusion.43
  323.3 0.2 fusion.107
  323.5 2.4 fusion.14
  325.9 13.0 %multiply_reduce_fusion = (f32[2]{0:T(128)S(1)}, f32[2,2048]{1,0:T(2,128)S(1)}) fusion(bf16[16,512,2048]{2,1,0:T(8,128)(2,1)} %bitcast.86, bf16[2,16,512]{2,1,0:T(8,128)(2,1)S(1)} %slice.75, bf16[2,2048]{1,0:T(2,128)(2,1)S(1)} %get-tuple-element.6), kind=kOutput, calls=%fused_computation.91 | convolution fusion | flops 67133440 | bytes 33611784 | tf_op jit(solution)/shard_map/bhc,hcd->bd/dot_general | solution.py:30
  338.9 0.7 fusion.97
  339.6 0.0 all-gather.7.cloned.1.call-update
  339.6 0.0 all-reduce.7.cloned.1.call-start
  339.6 61.9 %all-gather.7.cloned.1.call-done = bf16[128,2,2048]{2,1,0:T(2,128)(2,1)} async-done(((bf16[1,2,2048]{2,1,0:T(2,128)(2,1)}), bf16[128,2,2048]{2,1,0:T(2,128)(2,1)}) %all-gather.7.cloned.1.call-update) | async-done | bytes 1048592 | tf_op jit(solution)/shard_map/all_gather | solution.py:41
  401.5 1.5 reshape.68
  403.0 0.5 fusion.55
  403.4 2.7 fusion.50
  406.1 0.0 all-reduce.7.cloned.1.call-update
  406.1 149.7 %all-reduce.7.cloned.1.call-done = f32[256,2048]{1,0:T(8,128)} async-done(((f32[256,2048]{1,0:T(8,128)}), f32[256,2048]{1,0:T(8,128)}) %all-reduce.7.cloned.1.call-update) | async-done | bytes 2097168
  555.9 1.5 fusion.90
  (7 shorter events, 0.1 us)
Async XLA Ops:
  6.5 144.6 %all-gather.5.cloned.1.call-start = ((), (), s32[]{:S(2)}) async-start(), calls=%async_computation | async-start | bytes 1056768 | tf_op jit(solution)/shard_map/all_gather | solution.py:41
  8.2 14.5 %copy-start.5 = (s32[2]{0:T(128)S(1)}, s32[2]{0:T(128)}, u32[]{:S(2)}) copy-start(s32[2]{0:T(128)} %param.11) | copy-start | bytes 28
  27.4 43.5 %copy-start.3 = (bf16[2,2048]{1,0:T(2,128)(2,1)S(1)}, bf16[2,2048]{1,0:T(2,128)(2,1)}, u32[]{:S(2)}) copy-start(bf16[2,2048]{1,0:T(2,128)(2,1)} %param.10) | copy-start | bytes 24580
  71.0 13.2 %copy-start.4 = (f32[2,2048]{1,0:T(2,128)S(1)}, f32[2,2048]{1,0:T(2,128)}, u32[]{:S(2)}) copy-start(f32[2,2048]{1,0:T(2,128)} %param.14) | copy-start | bytes 49156
  71.0 81.7 %copy-start = (bf16[2,2048,88]{1,2,0:T(8,128)(2,1)S(1)}, bf16[2,2048,88]{1,2,0:T(8,128)(2,1)}, u32[]{:S(2)}) copy-start(bf16[2,2048,88]{1,2,0:T(8,128)(2,1)} %param.18) | copy-start | bytes 2162692
  71.0 82.1 %copy-start.1 = (bf16[2,88,2048]{2,1,0:T(8,128)(2,1)S(1)}, bf16[2,88,2048]{2,1,0:T(8,128)(2,1)}, u32[]{:S(2)}) copy-start(bf16[2,88,2048]{2,1,0:T(8,128)(2,1)} %param.19) | copy-start | bytes 2162692
  71.0 82.1 %copy-start.2 = (bf16[2,2048,88]{1,2,0:T(8,128)(2,1)S(1)}, bf16[2,2048,88]{1,2,0:T(8,128)(2,1)}, u32[]{:S(2)}) copy-start(bf16[2,2048,88]{1,2,0:T(8,128)(2,1)} %param.17) | copy-start | bytes 2162692
  84.9 220.8 %all-reduce.5.cloned.1.call-start = ((), (), s32[]{:S(2)}) async-start(), calls=%async_computation.2 | async-start | bytes 4194304
  155.9 245.6 %all-gather.7.cloned.1.call-start = ((), (), s32[]{:S(2)}) async-start(), calls=%async_computation.1 | async-start | bytes 1056768 | tf_op jit(solution)/shard_map/all_gather | solution.py:41
  339.6 216.3 %all-reduce.7.cloned.1.call-start = ((), (), s32[]{:S(2)}) async-start(), calls=%async_computation.3 | async-start | bytes 4194304
Sparse Core Ops, SparseCore 0:
  85.0 66.1 all-gather.4
  156.1 149.5 all-reduce.4
  339.7 61.7 all-gather.6
  406.3 149.5 all-reduce.6
where the time goes:
time: 565 us; the launch traced here: 564 us
  waiting for transfers between devices  427 us (76%)
  matrix products  70.2 us (12%)
  local copies, waits for them, and re-layouts  47.5 us (8%)
  between operations  13.3 us (2%)
    unnamed x6, waiting for transfers between devices  299 us
    all_gather x2, waiting for transfers between devices, local_step(): gathered = lax.all_gather(normed, 'dp', axis=0, tiled=True)  128 us
    slice x1, local copies, waits for them, and re-layouts, local_step(): w_attn_out[layer_idx]  43.5 us
    dot_general x2, matrix products, local_attention(): jnp.dot(normed, wq_l, preferred_element_type=jnp.float32)  28.7 us
    dot_general x2, matrix products, local_attention(): jnp.einsum('bhc,hcd->bd', mixed, wo_l.reshape(heads, latent, d_model), pr...  26.1 us
  transfers between devices with their start and end apart: 4, of which 4 were waited for; matrix products, arithmetic and copies ran while one was open for 0% of the time, Pallas kernels for 0%

commit v1 on v0

v1 whole, which is shorter than its diff:
```python
import functools

import jax
import jax.numpy as jnp
from jax import lax
from jax.experimental import pallas as pl
from jax.experimental.pallas import tpu as pltpu
from jax.sharding import PartitionSpec as P

NORM_EPS = 1e-6
MESH = pl.DeviceIdType.MESH
F32 = jnp.float32
BF16 = jnp.bfloat16


def dot(a, b):
    return jnp.dot(a, b, preferred_element_type=F32)


def dot_nt(a, b):
    return lax.dot_general(a, b, (((1,), (1,)), ((), ())), preferred_element_type=F32)


def kernel(
    cfg,
    x_ref, len_ref, ag_ref, fg_ref, cache_hbm, wq_hbm, wo_hbm, wu_hbm, wg_hbm, wd_hbm,
    out_ref,
    wq, wo, cbuf, wu, wg, wd,
    xsend, xrecv, qrow, qsend, qbuf, obuf, osend, orecv, lhs, ysend, yrecv, xh,
    p1, ga, gb, dsend, drecv, sa, sb, r1a, r1b, ta, tb, r2a, r2b, u3, r3,
    wq_sem, wo_sem, c_sem, f_sem, ssem, rsem,
):
    side, layers, heads, kv, latent, seq, d_model, q_chunk = cfg
    half, quarter = d_model // 2, d_model // 4
    heads_half = heads // 2
    qw = heads_half * kv
    n_q = qw // q_chunk
    scale = (3 * (kv - latent)) ** -0.5

    me = lax.axis_index('dp')
    core = lax.rem(me, 2)
    chip = lax.div(me, 2)
    cx = lax.rem(chip, side)
    cy = lax.rem(lax.div(chip, side), side)
    cz = lax.div(chip, side * side)
    other = 1 - core

    def device(z, y, x, k):
        return {'dp': ((z * side + y) * side + x) * 2 + k}

    def step(c, d):
        return lax.rem(c + d, side)

    partner = device(cz, cy, cx, other)
    x_peer = {d: device(cz, cy, step(cx, d), core) for d in range(1, side)}
    y_peer = {d: device(cz, step(cy, d), cx, core) for d in range(1, side)}
    z_peer = {d: device(step(cz, d), cy, cx, core) for d in range(1, side)}

    def wq_copy(layer, i):
        cols = pl.ds(pl.multiple_of(core * qw + i * q_chunk, 128), q_chunk)
        return pltpu.make_async_copy(wq_hbm.at[layer, :, cols], wq.at[i], wq_sem.at[i])

    def wo_copy(layer, i):
        rows = pl.ds(pl.multiple_of((core * heads_half + i) * latent, 128), latent)
        return pltpu.make_async_copy(wo_hbm.at[layer, rows, :], wo.at[i], wo_sem.at[i])

    def cache_copy(layer, b):
        return pltpu.make_async_copy(cache_hbm.at[layer, b], cbuf.at[b], c_sem.at[b])

    def ffn_copies(layer):
        return [
            pltpu.make_async_copy(wg_hbm.at[layer], wg.at[layer], f_sem.at[layer, 0]),
            pltpu.make_async_copy(wu_hbm.at[layer], wu.at[layer], f_sem.at[layer, 1]),
            pltpu.make_async_copy(wd_hbm.at[layer], wd.at[layer], f_sem.at[layer, 2]),
        ]

    for i in range(n_q):
        wq_copy(0, i).start()
    for b in range(2):
        cache_copy(0, b).start()
    for i in range(heads_half):
        wo_copy(0, i).start()
    for layer in range(layers):
        for copy in ffn_copies(layer):
            copy.start()

    barrier = pltpu.get_barrier_semaphore()
    peers = [partner, *x_peer.values(), *y_peer.values(), *z_peer.values()]
    for peer in peers:
        pl.semaphore_signal(barrier, inc=1, device_id=peer, device_id_type=MESH)
    pl.semaphore_wait(barrier, len(peers))

    lhs[:, 4:8, :] = jnp.zeros((heads_half, 4, latent), F32)
    pending = []

    def remote(layer, index, src, dst, peer):
        return pltpu.make_async_remote_copy(
            src_ref=src, dst_ref=dst, send_sem=ssem.at[layer, index], recv_sem=rsem.at[layer, index],
            device_id=peer, device_id_type=MESH)

    def send(layer, index, src, dst, peer):
        copy = remote(layer, index, src, dst, peer)
        copy.start()
        pending.append(copy)

    def recv(layer, index, dst, peer):
        remote(layer, index, dst, dst, peer).wait_recv()

    def rms(rows, gain):
        mean_sq = jnp.mean(rows * rows, axis=-1, keepdims=True)
        return rows * lax.rsqrt(mean_sq + NORM_EPS) * gain

    def swap(rows):
        return jnp.concatenate([rows[2:4], rows[0:2]], axis=0)

    def attention(layer, x4):
        normed = rms(x4, ag_ref[layer:layer + 1, :])
        h8 = jnp.concatenate([normed, normed], axis=0).astype(BF16)

        def q_step(i, carry):
            wq_copy(layer, i).wait()
            qrow[:, pl.ds(pl.multiple_of(i * q_chunk, 128), q_chunk)] = dot(h8, wq[i])
            return carry

        lax.fori_loop(0, n_q, q_step, 0)
        if layer + 1 < layers:
            for i in range(n_q):
                wq_copy(layer + 1, i).start()
        pair = 2 * kv
        for j in range(heads_half // 2):
            block = qrow[:, j * pair:(j + 1) * pair]
            odd = pltpu.roll(block[:, latent:latent + 640], 640 - 64, 1)
            for parity, q8 in ((0, block[:, :640]), (1, odd)):
                h = 2 * j + parity
                for b in range(2):
                    qbuf[layer, core, b, h:h + 1, :] = q8[b:b + 1, :]
                    qsend[layer, b, h:h + 1, :] = q8[2 + b:3 + b, :]
        send(layer, 1, qsend.at[layer], qbuf.at[layer, core], partner)
        recv(layer, 1, qbuf.at[layer, other], partner)

        for b in range(2):
            cache_copy(layer, b).wait()
            q = jnp.concatenate([qbuf[layer, 0, b], qbuf[layer, 1, b]], axis=0)[:, :kv].astype(BF16)
            s = dot(q, cbuf[b]) * scale
            positions = lax.broadcasted_iota(jnp.int32, (heads, seq), 1)
            s = jnp.where(positions < len_ref[b], s, -jnp.inf)
            e = jnp.exp(s - jnp.max(s, axis=-1, keepdims=True))
            p = (e / jnp.sum(e, axis=-1, keepdims=True)).astype(BF16)
            o = dot_nt(p, cbuf[b, :latent, :])
            obuf[b, 0] = o[:heads_half]
            obuf[b, 1] = o[heads_half:]
        if layer + 1 < layers:
            for b in range(2):
                cache_copy(layer + 1, b).start()
        for b in range(2):
            mine = obuf[b, core]
            theirs = obuf[b, other]
            for h in range(heads_half):
                lhs[h, b:b + 1, :] = mine[h:h + 1, :]
                osend[layer, h, b:b + 1, :] = theirs[h:h + 1, :]
        send(layer, 2, osend.at[layer], orecv.at[layer], partner)
        recv(layer, 2, orecv.at[layer], partner)
        for h in range(heads_half):
            lhs[h, 2:4, :] = orecv[layer, h]

        def o_step(i, acc):
            wo_copy(layer, i).wait()
            return acc + dot(lhs[i].astype(BF16), wo[i])

        acc = lax.fori_loop(0, heads_half, o_step, jnp.zeros((8, d_model), F32))
        if layer + 1 < layers:
            for i in range(heads_half):
                wo_copy(layer + 1, i).start()
        y4 = acc[0:4]
        ysend[layer] = y4
        send(layer, 3, ysend.at[layer], yrecv.at[layer], partner)
        recv(layer, 3, yrecv.at[layer], partner)
        return (x4 + (y4 + swap(yrecv[layer]))).astype(BF16).astype(F32)

    def ffn(layer, x4):
        g4 = rms(x4, fg_ref[layer:layer + 1, :]).astype(BF16)
        p1[layer, cx] = jnp.where(core == 0, g4[:, :half], g4[:, half:])
        for d in range(1, side):
            send(layer, 4 + d, p1.at[layer, cx], p1.at[layer, cx], x_peer[d])
        for d in range(1, side):
            recv(layer, 4 + d, p1.at[layer, step(cx, side - d)], x_peer[d])
        block = jnp.concatenate([p1[layer, i].astype(F32) for i in range(side)], axis=0).astype(BF16)
        ga[layer, core, cz, cy] = block[:, :quarter]
        gb[layer, core, cz, cy] = block[:, quarter:]
        for d in range(1, side):
            send(layer, 7 + d, ga.at[layer, core, cz, cy], ga.at[layer, core, cz, cy], y_peer[d])
        for d in range(1, side):
            send(layer, 10 + d, gb.at[layer, core, cz, cy], gb.at[layer, core, cz, cy], z_peer[d])
        for d in range(1, side):
            recv(layer, 7 + d, ga.at[layer, core, cz, step(cy, side - d)], y_peer[d])
        own_a = ga.at[layer, core, cz]
        for d in range(1, side):
            send(layer, 13 + d, own_a, own_a, z_peer[d])
        send(layer, 20, own_a, own_a, partner)
        for d in range(1, side):
            recv(layer, 10 + d, gb.at[layer, core, step(cz, side - d), cy], z_peer[d])
        own_b = gb.at[layer, core, :, cy]
        for d in range(1, side):
            send(layer, 16 + d, own_b, own_b, y_peer[d])
        send(layer, 24, own_b, own_b, partner)
        for d in range(1, side):
            got_a = ga.at[layer, core, step(cz, side - d)]
            recv(layer, 13 + d, got_a, z_peer[d])
            send(layer, 20 + d, got_a, got_a, partner)
            got_b = gb.at[layer, core, :, step(cy, side - d)]
            recv(layer, 16 + d, got_b, y_peer[d])
            send(layer, 24 + d, got_b, got_b, partner)
        for copy in ffn_copies(layer):
            copy.wait()

        rows = 4 * side ** 3

        def product(w, k):
            part_a = ga[layer, k].reshape(rows, quarter)
            part_b = gb[layer, k].reshape(rows, quarter)
            base = pl.multiple_of(k * half, 128)
            w_a = w[layer, :, pl.ds(base, quarter)]
            w_b = w[layer, :, pl.ds(base + quarter, quarter)]
            return dot_nt(part_a, w_a) + dot_nt(part_b, w_b)

        gate = product(wg, core)
        up = product(wu, core)
        for d in range(side):
            recv(layer, 20 + d, ga.at[layer, other, step(cz, side - d)], partner)
            recv(layer, 24 + d, gb.at[layer, other, :, step(cy, side - d)], partner)
        gate = gate + product(wg, other)
        up = up + product(wu, other)
        hidden = (jax.nn.silu(gate) * up).astype(BF16)

        shape = (side, side, 4 * side, quarter)
        for c in range(2):
            cols = pl.ds(pl.multiple_of(other * half + c * quarter, 128), quarter)
            dsend[layer, c] = dot(hidden, wd[layer, :, cols]).reshape(shape)
            send(layer, 28 + c, dsend.at[layer, c], drecv.at[layer, c], partner)
        for c, s in ((0, sa), (1, sb)):
            cols = pl.ds(pl.multiple_of(core * half + c * quarter, 128), quarter)
            s[layer] = dot(hidden, wd[layer, :, cols]).reshape(shape)
        for c, s in ((0, sa), (1, sb)):
            recv(layer, 28 + c, drecv.at[layer, c], partner)
            s[layer] = s[layer] + drecv[layer, c]
            for d in range(1, side):
                if c == 0:
                    send(layer, 29 + d, sa.at[layer, step(cz, d)], r1a.at[layer, d - 1], z_peer[d])
                else:
                    send(layer, 32 + d, sb.at[layer, :, step(cy, d)], r1b.at[layer, d - 1], y_peer[d])
        total = sa[layer, cz]
        for d in range(1, side):
            recv(layer, 29 + d, r1a.at[layer, d - 1], z_peer[d])
            total = total + r1a[layer, d - 1]
        ta[layer] = total
        for d in range(1, side):
            send(layer, 35 + d, ta.at[layer, step(cy, d)], r2a.at[layer, d - 1], y_peer[d])
        total = sb[layer, :, cy]
        for d in range(1, side):
            recv(layer, 32 + d, r1b.at[layer, d - 1], y_peer[d])
            total = total + r1b[layer, d - 1]
        tb[layer] = total
        for d in range(1, side):
            send(layer, 38 + d, tb.at[layer, step(cz, d)], r2b.at[layer, d - 1], z_peer[d])
        total = ta[layer, cy]
        for d in range(1, side):
            recv(layer, 35 + d, r2a.at[layer, d - 1], y_peer[d])
            total = total + r2a[layer, d - 1]
        for i in range(side):
            u3[layer, i, :, :quarter] = total[4 * i:4 * i + 4]
        total = tb[layer, cz]
        for d in range(1, side):
            recv(layer, 38 + d, r2b.at[layer, d - 1], z_peer[d])
            total = total + r2b[layer, d - 1]
        for i in range(side):
            u3[layer, i, :, quarter:] = total[4 * i:4 * i + 4]
        for d in range(1, side):
            send(layer, 41 + d, u3.at[layer, step(cx, d)], r3.at[layer, d - 1], x_peer[d])
        total = u3[layer, cx]
        for d in range(1, side):
            recv(layer, 41 + d, r3.at[layer, d - 1], x_peer[d])
            total = total + r3[layer, d - 1]
        kept = jnp.where(core == 0, x4[:, :half], x4[:, half:])
        xh[layer, core] = (kept + total).astype(BF16).astype(F32)
        send(layer, 45, xh.at[layer, core], xh.at[layer, core], partner)
        recv(layer, 45, xh.at[layer, other], partner)
        return jnp.concatenate([xh[layer, 0], xh[layer, 1]], axis=1)

    def reorder(x4):
        return jnp.where(core == 0, x4, swap(x4))

    xsend[...] = x_ref[...].astype(F32)
    send(0, 0, xsend, xrecv, partner)
    recv(0, 0, xrecv, partner)
    x4 = jnp.concatenate([xsend[...], xrecv[...]], axis=0)
    for layer in range(layers):
        x4 = attention(layer, x4)
        x4 = ffn(layer, reorder(x4))
        x4 = reorder(x4)
    out_ref[...] = x4[0:2].astype(BF16)
    for copy in pending:
        copy.wait_send()


def solution(mesh):
    devices = mesh.shape['dp']
    side = round((devices // 2) ** (1 / 3))

    def local_step(x, lengths, cache, attn_gain, ffn_gain, w_query, w_attn_out, w_up, w_gate, w_down):
        layers, _, seq, kv = cache.shape
        d_model = x.shape[1]
        heads = w_query.shape[2] // kv
        latent = w_attn_out.shape[1] // heads
        hid = w_up.shape[2]
        half, quarter, hh = d_model // 2, d_model // 4, heads // 2
        q_chunk = 512
        n_q = hh * kv // q_chunk
        blk = 4 * side
        cfg = (side, layers, heads, kv, latent, seq, d_model, q_chunk)
        vmem = pl.BlockSpec(memory_space=pltpu.VMEM)
        smem = pl.BlockSpec(memory_space=pltpu.SMEM)
        hbm = pl.BlockSpec(memory_space=pl.ANY)
        scratch = [
            pltpu.VMEM((n_q, d_model, q_chunk), BF16),
            pltpu.VMEM((hh, latent, d_model), BF16),
            pltpu.VMEM((2, kv, seq), BF16),
            pltpu.VMEM((layers, hid, d_model), BF16),
            pltpu.VMEM((layers, hid, d_model), BF16),
            pltpu.VMEM((layers, hid, d_model), BF16),
            pltpu.VMEM((2, d_model), F32),
            pltpu.VMEM((2, d_model), F32),
            pltpu.VMEM((8, hh * kv), F32),
            pltpu.VMEM((layers, 2, hh, 640), F32),
            pltpu.VMEM((layers, 2, 2, hh, 640), F32),
            pltpu.VMEM((2, 2, hh, latent), F32),
            pltpu.VMEM((layers, hh, 2, latent), F32),
            pltpu.VMEM((layers, hh, 2, latent), F32),
            pltpu.VMEM((hh, 8, latent), F32),
            pltpu.VMEM((layers, 4, d_model), F32),
            pltpu.VMEM((layers, 4, d_model), F32),
            pltpu.VMEM((layers, 2, 4, half), F32),
            pltpu.VMEM((layers, side, 4, half), BF16),
            pltpu.VMEM((layers, 2, side, side, blk, quarter), BF16),
            pltpu.VMEM((layers, 2, side, side, blk, quarter), BF16),
            pltpu.VMEM((layers, 2, side, side, blk, quarter), F32),
            pltpu.VMEM((layers, 2, side, side, blk, quarter), F32),
            pltpu.VMEM((layers, side, side, blk, quarter), F32),
            pltpu.VMEM((layers, side, side, blk, quarter), F32),
            pltpu.VMEM((layers, side - 1, side, blk, quarter), F32),
            pltpu.VMEM((layers, side - 1, side, blk, quarter), F32),
            pltpu.VMEM((layers, side, blk, quarter), F32),
            pltpu.VMEM((layers, side, blk, quarter), F32),
            pltpu.VMEM((layers, side - 1, blk, quarter), F32),
            pltpu.VMEM((layers, side - 1, blk, quarter), F32),
            pltpu.VMEM((layers, side, 4, half), F32),
            pltpu.VMEM((layers, side - 1, 4, half), F32),
            pltpu.SemaphoreType.DMA((n_q,)),
            pltpu.SemaphoreType.DMA((hh,)),
            pltpu.SemaphoreType.DMA((2,)),
            pltpu.SemaphoreType.DMA((layers, 3)),
            pltpu.SemaphoreType.DMA((layers, 46)),
            pltpu.SemaphoreType.DMA((layers, 46)),
        ]
        return pl.pallas_call(
            functools.partial(kernel, cfg),
            out_shape=jax.ShapeDtypeStruct(x.shape, BF16),
            in_specs=[vmem, smem, vmem, vmem, hbm, hbm, hbm, hbm, hbm, hbm],
            out_specs=vmem,
            scratch_shapes=scratch,
            compiler_params=pltpu.CompilerParams(
                collective_id=0, has_side_effects=True, vmem_limit_bytes=66_000_000),
            name='mla_decode',
        )(x, lengths, attn_gain, ffn_gain, jnp.swapaxes(cache, 2, 3), w_query, w_attn_out,
          jnp.swapaxes(w_up, 1, 2), jnp.swapaxes(w_gate, 1, 2), w_down)

    rows = ('replica', 'dp')
    return jax.shard_map(
        local_step,
        mesh=mesh,
        in_specs=(P(rows, None), P(rows), P(None, rows, None, None), P(), P(), P(), P(),
                  P(None, None, 'dp'), P(None, None, 'dp'), P(None, 'dp', None)),
        out_specs=P(rows, None),
        check_vma=False,
    )
```

time: 565 us -> 107 us (0.19)
  waiting for transfers between devices: 427 us -> 0 us
  Pallas kernels: 0 us -> 104 us
  matrix products: 70.2 us -> 0 us
  local copies, waits for them, and re-layouts: 47.5 us -> 1.3 us
  between operations: 13.3 us -> 0.01 us
    unnamed x6 -> x0, waiting for transfers between devices: 299 us -> none
    all_gather x2 -> x0, waiting for transfers between devices: 128 us -> none  [local_step(): gathered = lax.all_gather(normed, 'dp', axis=0, tiled=True)]
    pallas_call x0 -> x1, Pallas kernels: none -> 104 us  [local_step(): pl.pallas_call(functools.partial(kernel, cfg), out_shape=jax.ShapeDtypeSt...]
    dot_general x12 -> x0, matrix products: 70.2 us -> none  [the longest x2 28.7 us: local_attention(): jnp.dot(normed, wq_l, preferred_element_type=jnp.float32)]
    slice x5 -> x0, local copies, waits for them, and re-layouts: 44.3 us -> none  [the longest x1 43.5 us: local_step(): w_attn_out[layer_idx]]
  transfers between devices with their start and end apart: 4 -> 0, of which waited for: 4 -> 0; matrix products, arithmetic and copies ran while one was open for 0% -> 0% of each run, Pallas kernels for 0% -> 0%
where the time goes in v1:
time: 107 us; the launch traced here: 106 us
  Pallas kernels  104 us (97%)
  local copies, waits for them, and re-layouts  1.3 us (1%)
    pallas_call x1, Pallas kernels, local_step(): pl.pallas_call(functools.partial(kernel, cfg), out_shape=jax.ShapeDtypeSt...  104 us

profile of v1, /device:TPU:0, one launch (start us, length us, event | category | flops | bytes accessed | tf_op | source)
XLA Modules:
  0.0 105.7 jit_solution(3099860398808601095)
XLA Ops:
  0.0 104.4 %mla_decode.1 = bf16[2,2048]{1,0:T(2,128)(2,1)} custom-call(bf16[2,2048]{1,0:T(2,128)(2,1)} %x_ref.1, s32[2]{0:T(128)} %len_ref.1, f32[2,2048]{1,0:T(2,128)} %ag_ref.1, f32[2,2048]{1,0:T(2,128)} %fg_ref.1, bf16[2,2,576,1024]{3,2,1,0:T(8,128)(2,1)} %bitcast.3, bf16[2,2048,9216]{2,1,0:T(8,128)(2,1)} %wq_hbm.1, bf16[2,8192,2048]{2,1,0:T(8,128)(2,1)} %wo_hbm.1, ...), custom_call_target="tpu_custom_call" | custom-call | tf_op jit(solution)/shard_map/mla_decode/pallas_call | solution.py:364
  104.4 1.3 %copy.12 = bf16[2,2048]{1,0:T(2,128)(2,1)} copy(bf16[2,2048]{1,0:T(2,128)(2,1)} %mla_decode.1) | data formatting | bytes 16384

commit v2 on v0

v2 whole, which is shorter than its diff:
```python
import functools

import jax
import jax.numpy as jnp
from jax import lax
from jax.experimental import pallas as pl
from jax.experimental.pallas import tpu as pltpu
from jax.sharding import PartitionSpec as P

NORM_EPS = 1e-6
MESH = pl.DeviceIdType.MESH
F32 = jnp.float32
BF16 = jnp.bfloat16
COLOURS = (('z', 'y', 'x'), ('x', 'z', 'y'), ('y', 'z', 'x'))


def dot(a, b):
    return jnp.dot(a, b, preferred_element_type=F32)


def dot_nt(a, b):
    return lax.dot_general(a, b, (((1,), (1,)), ((), ())), preferred_element_type=F32)


def colour_columns(d_model):
    tiles = d_model // 128
    widths = [128 * ((tiles + 2 - c) // 3) for c in range(3)]
    return [(sum(widths[:c]), widths[c]) for c in range(3)]


def kernel(
    cfg,
    x_hbm, len_hbm, ag_hbm, fg_hbm, cache_hbm, wq_hbm, wo_hbm, wu_hbm, wg_hbm, wd_hbm,
    out_ref,
    wq, wo, cbuf, wu, wg, wd,
    xin, lens, ag, fg, lbuf, xsend, xrecv, qrow, qbuf, lhs, ysend, yrecv, asm,
    p1a, p1b, p1c, g_a, g_b, g_c, s_a, s_b, s_c, r1a, r1b, r1c, u_a, u_b, u_c, r2a, r2b, r2c,
    wq_sem, wo_sem, c_sem, f_sem, in_sem, ssem, rsem, agp_s, agp_r, rsp_s, rsp_r,
):
    side, layers, heads, kv, latent, seq, d_model, q_chunk, o_chunk = cfg
    heads_half = heads // 2
    qw = heads_half * kv
    n_q = qw // q_chunk
    n_o = d_model // o_chunk
    kdim = heads_half * latent
    plane = side * side
    rows = 2 * side ** 3
    scale = (3 * (kv - latent)) ** -0.5
    columns = colour_columns(d_model)
    p1, g_buf, s_buf = (p1a, p1b, p1c), (g_a, g_b, g_c), (s_a, s_b, s_c)
    r1, u_buf, r2 = (r1a, r1b, r1c), (u_a, u_b, u_c), (r2a, r2b, r2c)

    me = lax.axis_index('dp')
    core = lax.rem(me, 2)
    chip = lax.div(me, 2)
    coord = {'x': lax.rem(chip, side), 'y': lax.rem(lax.div(chip, side), side), 'z': lax.div(chip, plane)}
    other = 1 - core

    def step(c, d):
        return lax.rem(c + d, side)

    def device(k=core, **shift):
        at = {a: step(coord[a], shift.get(a, 0)) for a in 'zyx'}
        return {'dp': ((at['z'] * side + at['y']) * side + at['x']) * 2 + k}

    partner = {'dp': chip * 2 + other}
    hops = lambda d: min(d, side - d)
    axis_shifts = sorted(range(1, side), key=hops, reverse=True)
    plane_shifts = sorted(
        [(i, j) for i in range(side) for j in range(side) if i or j],
        key=lambda s: hops(s[0]) + hops(s[1]), reverse=True)

    def wq_copy(layer, i):
        cols = pl.ds(pl.multiple_of(core * qw + i * q_chunk, 128), q_chunk)
        return pltpu.make_async_copy(wq_hbm.at[layer, :, cols], wq.at[i], wq_sem.at[i])

    def wo_copy(layer, i):
        depth = pl.ds(pl.multiple_of(core * kdim, 128), kdim)
        cols = pl.ds(pl.multiple_of(i * o_chunk, 128), o_chunk)
        return pltpu.make_async_copy(wo_hbm.at[layer, depth, cols], wo.at[i], wo_sem.at[i])

    def cache_copy(layer, b):
        return pltpu.make_async_copy(cache_hbm.at[layer, b], cbuf.at[layer, b], c_sem.at[layer, b])

    ffn_pairs = ((wg_hbm, wg), (wu_hbm, wu), (wd_hbm, wd))

    def ffn_copies(layer):
        return [
            pltpu.make_async_copy(src.at[layer], dst.at[layer, core], f_sem.at[layer, i])
            for i, (src, dst) in enumerate(ffn_pairs)]

    inputs = [
        pltpu.make_async_copy(src, dst, in_sem.at[i])
        for i, (src, dst) in enumerate(((x_hbm, xin), (len_hbm, lens), (ag_hbm, ag), (fg_hbm, fg)))]
    for copy in inputs:
        copy.start()
    for i in range(n_q):
        wq_copy(0, i).start()
    for b in range(2):
        cache_copy(0, b).start()
    for i in range(n_o):
        wo_copy(0, i).start()

    barrier = pltpu.get_barrier_semaphore()
    peers = [partner] + [
        device(**shift) for shift in
        [{a: d} for a in 'zyx' for d in range(1, side)]
        + [{a: d, b: e} for a, b in ('zy', 'zx', 'yx') for d in range(1, side) for e in range(1, side)]]
    for peer in peers:
        pl.semaphore_signal(barrier, inc=1, device_id=peer, device_id_type=MESH)
    pl.semaphore_wait(barrier, len(peers))

    pending = []

    def remote(layer, index, src, dst, peer):
        return pltpu.make_async_remote_copy(
            src_ref=src, dst_ref=dst, send_sem=ssem.at[layer, index], recv_sem=rsem.at[layer, index],
            device_id=peer, device_id_type=MESH)

    def send(layer, index, src, dst, peer):
        copy = remote(layer, index, src, dst, peer)
        copy.start()
        pending.append(copy)

    def recv(layer, index, dst, peer):
        remote(layer, index, dst, dst, peer).wait_recv()

    def send_weights(layer):
        for b in range(2):
            send(layer, 2 + b, cache_hbm.at[layer, b], cbuf.at[layer, 2 + b], partner)
        for i, (src, dst) in enumerate(ffn_pairs):
            send(layer, 4 + i, src.at[layer], dst.at[layer, core], partner)

    for copy in inputs:
        copy.wait()
    xsend[0] = xin[...].astype(F32)
    send(0, 0, xsend.at[0], xrecv.at[0], partner)
    for b in range(2):
        lbuf[0, b:b + 1, :] = jnp.full((1, 128), lens[b], jnp.int32).astype(F32)
    send(0, 7, lbuf.at[0], lbuf.at[1], partner)
    send_weights(0)
    for layer in range(layers):
        for copy in ffn_copies(layer):
            copy.start()
    lhs[4:8, :] = jnp.zeros((4, kdim), F32)

    def rms(v, gain):
        mean_sq = jnp.mean(v * v, axis=-1, keepdims=True)
        return v * lax.rsqrt(mean_sq + NORM_EPS) * gain

    def attention(layer, x2):
        recv(layer, 0, xrecv.at[layer], partner)
        if layer == 0:
            recv(0, 7, lbuf.at[1], partner)
        x4 = jnp.concatenate([x2, xrecv[layer]], axis=0)
        normed = rms(x4, ag[layer:layer + 1, :])
        h8 = jnp.concatenate([normed, normed], axis=0).astype(BF16)

        def q_step(i, carry):
            wq_copy(layer, i).wait()
            qrow[:, pl.ds(pl.multiple_of(i * q_chunk, 128), q_chunk)] = dot(h8, wq[i])
            return carry

        lax.fori_loop(0, n_q, q_step, 0)
        if layer + 1 < layers:
            for i in range(n_q):
                wq_copy(layer + 1, i).start()
            for b in range(2):
                cache_copy(layer + 1, b).start()
            send_weights(layer + 1)
        pair = 2 * kv
        for j in range(heads_half // 2):
            block = qrow[:, j * pair:(j + 1) * pair]
            odd = pltpu.roll(block[:, latent:latent + 640], 640 - 64, 1)
            for parity, q8 in ((0, block[:, :640]), (1, odd)):
                h = 2 * j + parity
                for b in range(4):
                    qbuf[b, h:h + 1, :] = q8[b:b + 1, :]
        positions = lax.broadcasted_iota(jnp.int32, (heads_half, seq), 1).astype(F32)
        for b in range(2):
            cache_copy(layer, b).wait()
        for b in range(2):
            recv(layer, 2 + b, cbuf.at[layer, 2 + b], partner)
        for b in range(4):
            q = qbuf[b][:, :kv].astype(BF16)
            s = dot(q, cbuf[layer, b]) * scale
            length = lbuf[b // 2, b % 2:b % 2 + 1, 0:1]
            s = jnp.where(positions < length, s, -jnp.inf)
            e = jnp.exp(s - jnp.max(s, axis=-1, keepdims=True))
            p = (e / jnp.sum(e, axis=-1, keepdims=True)).astype(BF16)
            o = dot_nt(p, cbuf[layer, b, :latent, :])
            for h in range(heads_half):
                lhs[b:b + 1, h * latent:(h + 1) * latent] = o[h:h + 1, :]
        lhs_b = lhs[...].astype(BF16)

        def o_step(i, carry):
            wo_copy(layer, i).wait()
            y = dot(lhs_b, wo[i])
            cols = pl.ds(pl.multiple_of(i * o_chunk, 128), o_chunk)
            ysend[layer, 0, :, cols] = y[0:2]
            ysend[layer, 1, :, cols] = y[2:4]
            return carry

        lax.fori_loop(0, n_o, o_step, 0)
        send(layer, 1, ysend.at[layer, 1], yrecv.at[layer], partner)
        if layer + 1 < layers:
            for i in range(n_o):
                wo_copy(layer + 1, i).start()
        recv(layer, 1, yrecv.at[layer], partner)
        return (x2 + (ysend[layer, 0] + yrecv[layer])).astype(BF16).astype(F32)

    def slot(c):
        _, a, b = COLOURS[c]
        return coord[a] * side + coord[b]

    def plane_wait(buf, layer, send_sem, recv_sem, c, sent):
        part = buf.at[layer, pl.ds(0, plane - 1)]
        copy = pltpu.make_async_remote_copy(
            src_ref=part, dst_ref=part, send_sem=send_sem.at[layer, c], recv_sem=recv_sem.at[layer, c],
            device_id=partner, device_id_type=MESH)
        return copy.wait_send() if sent else copy.wait_recv()

    def natural_of(index):
        log = side.bit_length() - 1
        r = index & 1
        at = {'x': (index >> 1) & (side - 1), 'y': (index >> (1 + log)) & (side - 1), 'z': index >> (1 + 2 * log)}
        return [
            (((at[o] << (2 * log)) | (at[a] << log) | at[b]) << 1) | r for o, a, b in COLOURS]

    def ffn(layer, x2):
        g2 = rms(x2, fg[layer:layer + 1, :]).astype(BF16)
        for c, (base, width) in enumerate(columns):
            _, a, b = COLOURS[c]
            p1[c][layer, slot(c)] = g2[:, base:base + width]
            for i, j in plane_shifts:
                block = p1[c].at[layer, slot(c)]
                pltpu.make_async_remote_copy(
                    src_ref=block, dst_ref=block, send_sem=agp_s.at[layer, c], recv_sem=agp_r.at[layer, c],
                    device_id=device(**{a: i, b: j}), device_id_type=MESH).start()
        for c, (base, width) in enumerate(columns):
            axis = COLOURS[c][0]
            plane_wait(p1[c], layer, agp_s, agp_r, c, False)
            for i in range(plane):
                asm[2 * i:2 * i + 2, base:base + width] = p1[c][layer, i].astype(F32)
            g_buf[c][layer, coord[axis]] = asm[:, base:base + width].astype(BF16)
            own = g_buf[c].at[layer, coord[axis]]
            for d in axis_shifts:
                send(layer, 8 + 3 * c + d - 1, own, own, device(**{axis: d}))
        for copy in ffn_copies(layer):
            copy.wait()
        for i, (_, dst) in enumerate(ffn_pairs):
            recv(layer, 4 + i, dst.at[layer, other], partner)

        across = lax.broadcasted_iota(jnp.int32, (rows, rows), 1)
        down = lax.broadcasted_iota(jnp.int32, (rows, rows), 0)
        parts = []
        for c, (base, width) in enumerate(columns):
            axis = COLOURS[c][0]
            for d in axis_shifts:
                recv(layer, 8 + 3 * c + d - 1, g_buf[c].at[layer, step(coord[axis], side - d)], device(**{axis: d}))
            part = g_buf[c][layer].reshape(rows, width)
            if c:
                pick = (natural_of(down)[c] == across).astype(F32).astype(BF16)
                part = dot(pick, part).astype(BF16)
            parts.append(part)
        g = jnp.concatenate(parts, axis=1)
        hidden = []
        for k in range(2):
            gate = dot_nt(g, wg[layer, k])
            up = dot_nt(g, wu[layer, k])
            hidden.append((jax.nn.silu(gate) * up).astype(BF16))

        for c, (base, width) in enumerate(columns):
            axis = COLOURS[c][0]
            total = None
            for k in range(2):
                a = hidden[k]
                if c:
                    pick = (natural_of(across)[c] == down).astype(F32).astype(BF16)
                    a = dot(pick, a).astype(BF16)
                term = dot(a, wd[layer, k, :, base:base + width])
                total = term if total is None else total + term
            s_buf[c][layer] = total.reshape(side, 2 * plane, width)
            for d in axis_shifts:
                send(layer, 17 + 3 * c + d - 1, s_buf[c].at[layer, step(coord[axis], d)], r1[c].at[layer, d - 1],
                     device(**{axis: d}))
        for c, (base, width) in enumerate(columns):
            axis, a, b = COLOURS[c]
            total = s_buf[c][layer, coord[axis]]
            for d in axis_shifts:
                recv(layer, 17 + 3 * c + d - 1, r1[c].at[layer, d - 1], device(**{axis: d}))
                total = total + r1[c][layer, d - 1]
            for i in range(plane):
                u_buf[c][layer, i] = total[2 * i:2 * i + 2]
            for i, j in plane_shifts:
                target = step(coord[a], i) * side + step(coord[b], j)
                pltpu.make_async_remote_copy(
                    src_ref=u_buf[c].at[layer, target], dst_ref=r2[c].at[layer, slot(c)],
                    send_sem=rsp_s.at[layer, c], recv_sem=rsp_r.at[layer, c],
                    device_id=device(**{a: i, b: j}), device_id_type=MESH).start()
        sums = []
        for c in range(3):
            r2[c][layer, slot(c)] = u_buf[c][layer, slot(c)]
            plane_wait(r2[c], layer, rsp_s, rsp_r, c, False)
            total = r2[c][layer, 0]
            for i in range(1, plane):
                total = total + r2[c][layer, i]
            sums.append(total)
        return (x2 + jnp.concatenate(sums, axis=1)).astype(BF16).astype(F32)

    x2 = xsend[0]
    for layer in range(layers):
        x2 = attention(layer, x2)
        x2 = ffn(layer, x2)
        if layer + 1 < layers:
            xsend[layer + 1] = x2
            send(layer + 1, 0, xsend.at[layer + 1], xrecv.at[layer + 1], partner)
    out_ref[...] = x2
    for copy in pending:
        copy.wait_send()
    for layer in range(layers):
        for c in range(3):
            plane_wait(p1[c], layer, agp_s, agp_r, c, True)
            plane_wait(u_buf[c], layer, rsp_s, rsp_r, c, True)


def solution(mesh):
    devices = mesh.shape['dp']
    side = round((devices // 2) ** (1 / 3))

    def local_step(x, lengths, cache, attn_gain, ffn_gain, w_query, w_attn_out, w_up, w_gate, w_down):
        layers, _, seq, kv = cache.shape
        d_model = x.shape[1]
        heads = w_query.shape[2] // kv
        latent = w_attn_out.shape[1] // heads
        hid = w_up.shape[2]
        hh = heads // 2
        q_chunk, o_chunk = 512, 256
        n_q, n_o = hh * kv // q_chunk, d_model // o_chunk
        plane = side * side
        widths = [w for _, w in colour_columns(d_model)]
        cfg = (side, layers, heads, kv, latent, seq, d_model, q_chunk, o_chunk)
        hbm = pl.BlockSpec(memory_space=pl.ANY)
        scratch = [
            pltpu.VMEM((n_q, d_model, q_chunk), BF16),
            pltpu.VMEM((n_o, hh * latent, o_chunk), BF16),
            pltpu.VMEM((layers, 4, kv, seq), BF16),
            pltpu.VMEM((layers, 2, hid, d_model), BF16),
            pltpu.VMEM((layers, 2, hid, d_model), BF16),
            pltpu.VMEM((layers, 2, hid, d_model), BF16),
            pltpu.VMEM((2, d_model), BF16),
            pltpu.SMEM((2,), jnp.int32),
            pltpu.VMEM((layers, d_model), F32),
            pltpu.VMEM((layers, d_model), F32),
            pltpu.VMEM((2, 2, 128), F32),
            pltpu.VMEM((layers, 2, d_model), F32),
            pltpu.VMEM((layers, 2, d_model), F32),
            pltpu.VMEM((8, hh * kv), F32),
            pltpu.VMEM((4, hh, 640), F32),
            pltpu.VMEM((8, hh * latent), F32),
            pltpu.VMEM((layers, 2, 2, d_model), F32),
            pltpu.VMEM((layers, 2, d_model), F32),
            pltpu.VMEM((2 * plane, d_model), F32),
            *[pltpu.VMEM((layers, plane, 2, w), BF16) for w in widths],
            *[pltpu.VMEM((layers, side, 2 * plane, w), BF16) for w in widths],
            *[pltpu.VMEM((layers, side, 2 * plane, w), F32) for w in widths],
            *[pltpu.VMEM((layers, side - 1, 2 * plane, w), F32) for w in widths],
            *[pltpu.VMEM((layers, plane, 2, w), F32) for w in widths],
            *[pltpu.VMEM((layers, plane, 2, w), F32) for w in widths],
            pltpu.SemaphoreType.DMA((n_q,)),
            pltpu.SemaphoreType.DMA((n_o,)),
            pltpu.SemaphoreType.DMA((layers, 2)),
            pltpu.SemaphoreType.DMA((layers, 3)),
            pltpu.SemaphoreType.DMA((4,)),
            pltpu.SemaphoreType.DMA((layers, 26)),
            pltpu.SemaphoreType.DMA((layers, 26)),
            *[pltpu.SemaphoreType.DMA((layers, 3)) for _ in range(4)],
        ]
        out = pl.pallas_call(
            functools.partial(kernel, cfg),
            out_shape=jax.ShapeDtypeStruct(x.shape, F32),
            in_specs=[hbm] * 10,
            out_specs=pl.BlockSpec(memory_space=pltpu.VMEM),
            scratch_shapes=scratch,
            compiler_params=pltpu.CompilerParams(
                collective_id=0, has_side_effects=True, vmem_limit_bytes=66_500_000),
            name='mla_decode',
        )(x, lengths, attn_gain, ffn_gain, jnp.swapaxes(cache, 2, 3), w_query, w_attn_out,
          jnp.swapaxes(w_up, 1, 2), jnp.swapaxes(w_gate, 1, 2), w_down)
        return out.astype(BF16)

    rows = ('replica', 'dp')
    return jax.shard_map(
        local_step,
        mesh=mesh,
        in_specs=(P(rows, None), P(rows), P(None, rows, None, None), P(), P(), P(), P(),
                  P(None, None, 'dp'), P(None, None, 'dp'), P(None, 'dp', None)),
        out_specs=P(rows, None),
        check_vma=False,
    )
```

time: 565 us -> 84.3 us (0.15)
  waiting for transfers between devices: 427 us -> 0 us
  Pallas kernels: 0 us -> 82.8 us
  matrix products: 70.2 us -> 0 us
  local copies, waits for them, and re-layouts: 47.5 us -> 0 us
  between operations: 13.3 us -> 0.01 us
    unnamed x6 -> x0, waiting for transfers between devices: 299 us -> none
    all_gather x2 -> x0, waiting for transfers between devices: 128 us -> none  [local_step(): gathered = lax.all_gather(normed, 'dp', axis=0, tiled=True)]
    pallas_call x0 -> x1, Pallas kernels: none -> 82.8 us  [local_step(): pl.pallas_call(functools.partial(kernel, cfg), out_shape=jax.ShapeDtypeSt...]
    dot_general x12 -> x0, matrix products: 70.2 us -> none  [the longest x2 28.7 us: local_attention(): jnp.dot(normed, wq_l, preferred_element_type=jnp.float32)]
    slice x5 -> x0, local copies, waits for them, and re-layouts: 44.3 us -> none  [the longest x1 43.5 us: local_step(): w_attn_out[layer_idx]]
  transfers between devices with their start and end apart: 4 -> 0, of which waited for: 4 -> 0; matrix products, arithmetic and copies ran while one was open for 0% -> 0% of each run, Pallas kernels for 0% -> 0%
where the time goes in v2:
time: 84.3 us; the launch traced here: 84.1 us
  Pallas kernels  82.8 us (98%)
  other arithmetic  1.32 us (2%)
    pallas_call x1, Pallas kernels, local_step(): pl.pallas_call(functools.partial(kernel, cfg), out_shape=jax.ShapeDtypeSt...  82.8 us

profile of v2, /device:TPU:0, one launch (start us, length us, event | category | flops | bytes accessed | tf_op | source)
XLA Modules:
  0.0 84.1 jit_solution(17727220850928965562)
XLA Ops:
  0.0 82.8 %mla_decode.1 = f32[2,2048]{1,0:T(2,128)} custom-call(bf16[2,2048]{1,0:T(2,128)(2,1)} %x_hbm.1, s32[2]{0:T(128)} %len_hbm.1, f32[2,2048]{1,0:T(2,128)} %ag_hbm.1, f32[2,2048]{1,0:T(2,128)} %fg_hbm.1, bf16[2,2,576,1024]{3,2,1,0:T(8,128)(2,1)} %bitcast.3, bf16[2,2048,9216]{2,1,0:T(8,128)(2,1)} %wq_hbm.1, bf16[2,8192,2048]{2,1,0:T(8,128)(2,1)} %wo_hbm.1, ...), custom_call_target="tpu_custom_call" | custom-call | tf_op jit(solution)/shard_map/mla_decode/pallas_call | solution.py:379
  82.8 1.3 %convert_element_type.3 = bf16[2,2048]{1,0:T(2,128)(2,1)} convert(f32[2,2048]{1,0:T(2,128)} %mla_decode.1) | non-fusion elementwise | flops 4096 | bytes 24576 | tf_op jit(solution)/shard_map/convert_element_type | solution.py:390

commit v3 on v2

--- a/solution.py
+++ b/solution.py
@@ -94,10 +94,12 @@
         for i, (src, dst) in enumerate(((x_hbm, xin), (len_hbm, lens), (ag_hbm, ag), (fg_hbm, fg)))]
     for copy in inputs:
         copy.start()
+    for b in range(2):
+        cache_copy(0, b).start()
     for i in range(n_q):
         wq_copy(0, i).start()
-    for b in range(2):
-        cache_copy(0, b).start()
+    for copy in ffn_copies(0):
+        copy.start()
     for i in range(n_o):
         wo_copy(0, i).start()
 
@@ -125,11 +127,14 @@
     def recv(layer, index, dst, peer):
         remote(layer, index, dst, dst, peer).wait_recv()
 
-    def send_weights(layer):
+    def send_cache(layer, src):
         for b in range(2):
-            send(layer, 2 + b, cache_hbm.at[layer, b], cbuf.at[layer, 2 + b], partner)
+            send(layer, 2 + b, src.at[layer, b], cbuf.at[layer, 2 + b], partner)
+
+    def send_ffn(layer, local):
         for i, (src, dst) in enumerate(ffn_pairs):
-            send(layer, 4 + i, src.at[layer], dst.at[layer, core], partner)
+            src = dst.at[layer, core] if local else src.at[layer]
+            send(layer, 4 + i, src, dst.at[layer, core], partner)
 
     for copy in inputs:
         copy.wait()
@@ -138,10 +143,9 @@
     for b in range(2):
         lbuf[0, b:b + 1, :] = jnp.full((1, 128), lens[b], jnp.int32).astype(F32)
     send(0, 7, lbuf.at[0], lbuf.at[1], partner)
-    send_weights(0)
-    for layer in range(layers):
-        for copy in ffn_copies(layer):
-            copy.start()
+    for b in range(2):
+        cache_copy(0, b).wait()
+    send_cache(0, cbuf)
     lhs[4:8, :] = jnp.zeros((4, kdim), F32)
 
     def rms(v, gain):
@@ -162,12 +166,10 @@
             return carry
 
         lax.fori_loop(0, n_q, q_step, 0)
-        if layer + 1 < layers:
-            for i in range(n_q):
-                wq_copy(layer + 1, i).start()
-            for b in range(2):
-                cache_copy(layer + 1, b).start()
-            send_weights(layer + 1)
+        for copy in ffn_copies(layer):
+            copy.wait()
+        if layer == 0:
+            send_ffn(layer, True)
         pair = 2 * kv
         for j in range(heads_half // 2):
             block = qrow[:, j * pair:(j + 1) * pair]
@@ -177,8 +179,9 @@
                 for b in range(4):
                     qbuf[b, h:h + 1, :] = q8[b:b + 1, :]
         positions = lax.broadcasted_iota(jnp.int32, (heads_half, seq), 1).astype(F32)
-        for b in range(2):
-            cache_copy(layer, b).wait()
+        if layer:
+            for b in range(2):
+                cache_copy(layer, b).wait()
         for b in range(2):
             recv(layer, 2 + b, cbuf.at[layer, 2 + b], partner)
         for b in range(4):
@@ -204,6 +207,12 @@
         lax.fori_loop(0, n_o, o_step, 0)
         send(layer, 1, ysend.at[layer, 1], yrecv.at[layer], partner)
         if layer + 1 < layers:
+            for b in range(2):
+                cache_copy(layer + 1, b).start()
+            for copy in ffn_copies(layer + 1):
+                copy.start()
+            for i in range(n_q):
+                wq_copy(layer + 1, i).start()
             for i in range(n_o):
                 wo_copy(layer + 1, i).start()
         recv(layer, 1, yrecv.at[layer], partner)
@@ -237,6 +246,9 @@
                 pltpu.make_async_remote_copy(
                     src_ref=block, dst_ref=block, send_sem=agp_s.at[layer, c], recv_sem=agp_r.at[layer, c],
                     device_id=device(**{a: i, b: j}), device_id_type=MESH).start()
+        if layer + 1 < layers:
+            send_cache(layer + 1, cache_hbm)
+            send_ffn(layer + 1, False)
         for c, (base, width) in enumerate(columns):
             axis = COLOURS[c][0]
             plane_wait(p1[c], layer, agp_s, agp_r, c, False)
@@ -246,8 +258,6 @@
             own = g_buf[c].at[layer, coord[axis]]
             for d in axis_shifts:
                 send(layer, 8 + 3 * c + d - 1, own, own, device(**{axis: d}))
-        for copy in ffn_copies(layer):
-            copy.wait()
         for i, (_, dst) in enumerate(ffn_pairs):
             recv(layer, 4 + i, dst.at[layer, other], partner)
 
@@ -378,7 +388,7 @@
         ]
         out = pl.pallas_call(
             functools.partial(kernel, cfg),
-            out_shape=jax.ShapeDtypeStruct(x.shape, F32),
+            out_shape=pltpu.VMEM(x.shape, F32),
             in_specs=[hbm] * 10,
             out_specs=pl.BlockSpec(memory_space=pltpu.VMEM),
             scratch_shapes=scratch,

time: 84.3 us -> 82.6 us (0.980)
  Pallas kernels: 82.8 us -> 81.9 us
    pallas_call x1, Pallas kernels: 82.8 us -> 81.9 us  [local_step(): pl.pallas_call(functools.partial(kernel, cfg), out_shape=pltpu.VMEM(x.sha...]
where the time goes in v3:
time: 82.6 us; the launch traced here: 82.5 us
  Pallas kernels  81.9 us (99%)
    pallas_call x1, Pallas kernels, local_step(): pl.pallas_call(functools.partial(kernel, cfg), out_shape=pltpu.VMEM(x.sha...  81.9 us

profile of v3, /device:TPU:0, one launch (start us, length us, event | category | flops | bytes accessed | tf_op | source)
XLA Modules:
  0.0 82.5 jit_solution(4827107431398541644)
XLA Ops:
  0.0 81.9 %mla_decode.1 = f32[2,2048]{1,0:T(2,128)S(1)} custom-call(bf16[2,2048]{1,0:T(2,128)(2,1)} %x_hbm.1, s32[2]{0:T(128)} %len_hbm.1, f32[2,2048]{1,0:T(2,128)} %ag_hbm.1, f32[2,2048]{1,0:T(2,128)} %fg_hbm.1, bf16[2,2,576,1024]{3,2,1,0:T(8,128)(2,1)} %bitcast.3, bf16[2,2048,9216]{2,1,0:T(8,128)(2,1)} %wq_hbm.1, bf16[2,8192,2048]{2,1,0:T(8,128)(2,1)} %wo_hbm.1, ...), custom_call_target="tpu_custom_call" | custom-call | tf_op jit(solution)/shard_map/mla_decode/pallas_call | solution.py:389
  81.9 0.6 convert_element_type.3

commit v4 on v3

--- a/solution.py
+++ b/solution.py
@@ -33,7 +33,7 @@
     x_hbm, len_hbm, ag_hbm, fg_hbm, cache_hbm, wq_hbm, wo_hbm, wu_hbm, wg_hbm, wd_hbm,
     out_ref,
     wq, wo, cbuf, wu, wg, wd,
-    xin, lens, ag, fg, lbuf, xsend, xrecv, qrow, qbuf, lhs, ysend, yrecv, asm,
+    xin, lens, ag, fg, xsend, xrecv, qrow, qsend, qbuf, obuf, osend, orecv, lhs, ysend, yrecv, asm,
     p1a, p1b, p1c, g_a, g_b, g_c, s_a, s_b, s_c, r1a, r1b, r1c, u_a, u_b, u_c, r2a, r2b, r2c,
     wq_sem, wo_sem, c_sem, f_sem, in_sem, ssem, rsem, agp_s, agp_r, rsp_s, rsp_r,
 ):
@@ -94,10 +94,10 @@
         for i, (src, dst) in enumerate(((x_hbm, xin), (len_hbm, lens), (ag_hbm, ag), (fg_hbm, fg)))]
     for copy in inputs:
         copy.start()
+    for i in range(n_q):
+        wq_copy(0, i).start()
     for b in range(2):
         cache_copy(0, b).start()
-    for i in range(n_q):
-        wq_copy(0, i).start()
     for copy in ffn_copies(0):
         copy.start()
     for i in range(n_o):
@@ -127,25 +127,16 @@
     def recv(layer, index, dst, peer):
         remote(layer, index, dst, dst, peer).wait_recv()
 
-    def send_cache(layer, src):
-        for b in range(2):
-            send(layer, 2 + b, src.at[layer, b], cbuf.at[layer, 2 + b], partner)
-
-    def send_ffn(layer, local):
-        for i, (src, dst) in enumerate(ffn_pairs):
-            src = dst.at[layer, core] if local else src.at[layer]
-            send(layer, 4 + i, src, dst.at[layer, core], partner)
+    def send_ffn(layer, which):
+        for i in which:
+            src, dst = ffn_pairs[i]
+            send(layer, 4 + i, src.at[layer], dst.at[layer, core], partner)
 
     for copy in inputs:
         copy.wait()
     xsend[0] = xin[...].astype(F32)
     send(0, 0, xsend.at[0], xrecv.at[0], partner)
-    for b in range(2):
-        lbuf[0, b:b + 1, :] = jnp.full((1, 128), lens[b], jnp.int32).astype(F32)
-    send(0, 7, lbuf.at[0], lbuf.at[1], partner)
-    for b in range(2):
-        cache_copy(0, b).wait()
-    send_cache(0, cbuf)
+    send_ffn(0, (0, 1))
     lhs[4:8, :] = jnp.zeros((4, kdim), F32)
 
     def rms(v, gain):
@@ -154,8 +145,6 @@
 
     def attention(layer, x2):
         recv(layer, 0, xrecv.at[layer], partner)
-        if layer == 0:
-            recv(0, 7, lbuf.at[1], partner)
         x4 = jnp.concatenate([x2, xrecv[layer]], axis=0)
         normed = rms(x4, ag[layer:layer + 1, :])
         h8 = jnp.concatenate([normed, normed], axis=0).astype(BF16)
@@ -168,32 +157,40 @@
         lax.fori_loop(0, n_q, q_step, 0)
         for copy in ffn_copies(layer):
             copy.wait()
-        if layer == 0:
-            send_ffn(layer, True)
         pair = 2 * kv
         for j in range(heads_half // 2):
             block = qrow[:, j * pair:(j + 1) * pair]
             odd = pltpu.roll(block[:, latent:latent + 640], 640 - 64, 1)
             for parity, q8 in ((0, block[:, :640]), (1, odd)):
                 h = 2 * j + parity
-                for b in range(4):
-                    qbuf[b, h:h + 1, :] = q8[b:b + 1, :]
-        positions = lax.broadcasted_iota(jnp.int32, (heads_half, seq), 1).astype(F32)
-        if layer:
-            for b in range(2):
-                cache_copy(layer, b).wait()
+                for b in range(2):
+                    qbuf[layer, core, b, h:h + 1, :] = q8[b:b + 1, :]
+                    qsend[layer, b, h:h + 1, :] = q8[2 + b:3 + b, :]
+        send(layer, 2, qsend.at[layer], qbuf.at[layer, core], partner)
+        positions = lax.broadcasted_iota(jnp.int32, (heads, seq), 1)
         for b in range(2):
-            recv(layer, 2 + b, cbuf.at[layer, 2 + b], partner)
-        for b in range(4):
-            q = qbuf[b][:, :kv].astype(BF16)
+            cache_copy(layer, b).wait()
+        recv(layer, 2, qbuf.at[layer, other], partner)
+        for b in range(2):
+            q = jnp.concatenate([qbuf[layer, 0, b], qbuf[layer, 1, b]], axis=0)[:, :kv].astype(BF16)
             s = dot(q, cbuf[layer, b]) * scale
-            length = lbuf[b // 2, b % 2:b % 2 + 1, 0:1]
-            s = jnp.where(positions < length, s, -jnp.inf)
+            s = jnp.where(positions < lens[b], s, -jnp.inf)
             e = jnp.exp(s - jnp.max(s, axis=-1, keepdims=True))
             p = (e / jnp.sum(e, axis=-1, keepdims=True)).astype(BF16)
             o = dot_nt(p, cbuf[layer, b, :latent, :])
+            obuf[b, 0] = o[:heads_half]
+            obuf[b, 1] = o[heads_half:]
+        for b in range(2):
+            theirs = obuf[b, other]
             for h in range(heads_half):
-                lhs[b:b + 1, h * latent:(h + 1) * latent] = o[h:h + 1, :]
+                osend[layer, b:b + 1, h * latent:(h + 1) * latent] = theirs[h:h + 1, :]
+        send(layer, 3, osend.at[layer], orecv.at[layer], partner)
+        for b in range(2):
+            mine = obuf[b, core]
+            for h in range(heads_half):
+                lhs[b:b + 1, h * latent:(h + 1) * latent] = mine[h:h + 1, :]
+        recv(layer, 3, orecv.at[layer], partner)
+        lhs[2:4, :] = orecv[layer]
         lhs_b = lhs[...].astype(BF16)
 
         def o_step(i, carry):
@@ -206,6 +203,8 @@
 
         lax.fori_loop(0, n_o, o_step, 0)
         send(layer, 1, ysend.at[layer, 1], yrecv.at[layer], partner)
+        if layer == 0:
+            send_ffn(0, (2,))
         if layer + 1 < layers:
             for b in range(2):
                 cache_copy(layer + 1, b).start()
@@ -247,8 +246,7 @@
                     src_ref=block, dst_ref=block, send_sem=agp_s.at[layer, c], recv_sem=agp_r.at[layer, c],
                     device_id=device(**{a: i, b: j}), device_id_type=MESH).start()
         if layer + 1 < layers:
-            send_cache(layer + 1, cache_hbm)
-            send_ffn(layer + 1, False)
+            send_ffn(layer + 1, (0, 1, 2))
         for c, (base, width) in enumerate(columns):
             axis = COLOURS[c][0]
             plane_wait(p1[c], layer, agp_s, agp_r, c, False)
@@ -354,7 +352,7 @@
         scratch = [
             pltpu.VMEM((n_q, d_model, q_chunk), BF16),
             pltpu.VMEM((n_o, hh * latent, o_chunk), BF16),
-            pltpu.VMEM((layers, 4, kv, seq), BF16),
+            pltpu.VMEM((layers, 2, kv, seq), BF16),
             pltpu.VMEM((layers, 2, hid, d_model), BF16),
             pltpu.VMEM((layers, 2, hid, d_model), BF16),
             pltpu.VMEM((layers, 2, hid, d_model), BF16),
@@ -362,11 +360,14 @@
             pltpu.SMEM((2,), jnp.int32),
             pltpu.VMEM((layers, d_model), F32),
             pltpu.VMEM((layers, d_model), F32),
-            pltpu.VMEM((2, 2, 128), F32),
             pltpu.VMEM((layers, 2, d_model), F32),
             pltpu.VMEM((layers, 2, d_model), F32),
             pltpu.VMEM((8, hh * kv), F32),
-            pltpu.VMEM((4, hh, 640), F32),
+            pltpu.VMEM((layers, 2, hh, 640), F32),
+            pltpu.VMEM((layers, 2, 2, hh, 640), F32),
+            pltpu.VMEM((2, 2, hh, latent), F32),
+            pltpu.VMEM((layers, 2, hh * latent), F32),
+            pltpu.VMEM((layers, 2, hh * latent), F32),
             pltpu.VMEM((8, hh * latent), F32),
             pltpu.VMEM((layers, 2, 2, d_model), F32),
             pltpu.VMEM((layers, 2, d_model), F32),

time: 82.6 us -> 83.7 us (1.013)
  Pallas kernels: 81.9 us -> 82.9 us
    pallas_call x1, Pallas kernels: 81.9 us -> 82.9 us  [local_step(): pl.pallas_call(functools.partial(kernel, cfg), out_shape=pltpu.VMEM(x.sha...]
where the time goes in v4:
time: 83.7 us; the launch traced here: 83.6 us
  Pallas kernels  82.9 us (99%)
    pallas_call x1, Pallas kernels, local_step(): pl.pallas_call(functools.partial(kernel, cfg), out_shape=pltpu.VMEM(x.sha...  82.9 us

profile of v4, /device:TPU:0, one launch (start us, length us, event | category | flops | bytes accessed | tf_op | source)
XLA Modules:
  0.0 83.6 jit_solution(15090644766274415551)
XLA Ops:
  0.0 82.9 %mla_decode.1 = f32[2,2048]{1,0:T(2,128)S(1)} custom-call(bf16[2,2048]{1,0:T(2,128)(2,1)} %x_hbm.1, s32[2]{0:T(128)} %len_hbm.1, f32[2,2048]{1,0:T(2,128)} %ag_hbm.1, f32[2,2048]{1,0:T(2,128)} %fg_hbm.1, bf16[2,2,576,1024]{3,2,1,0:T(8,128)(2,1)} %bitcast.3, bf16[2,2048,9216]{2,1,0:T(8,128)(2,1)} %wq_hbm.1, bf16[2,8192,2048]{2,1,0:T(8,128)(2,1)} %wo_hbm.1, ...), custom_call_target="tpu_custom_call" | custom-call | tf_op jit(solution)/shard_map/mla_decode/pallas_call | solution.py:390
  82.9 0.6 convert_element_type.3

commit v5 on v3

--- a/solution.py
+++ b/solution.py
@@ -43,6 +43,7 @@
     n_q = qw // q_chunk
     n_o = d_model // o_chunk
     kdim = heads_half * latent
+    early = n_o - 3
     plane = side * side
     rows = 2 * side ** 3
     scale = (3 * (kv - latent)) ** -0.5
@@ -98,10 +99,6 @@
         cache_copy(0, b).start()
     for i in range(n_q):
         wq_copy(0, i).start()
-    for copy in ffn_copies(0):
-        copy.start()
-    for i in range(n_o):
-        wo_copy(0, i).start()
 
     barrier = pltpu.get_barrier_semaphore()
     peers = [partner] + [
@@ -162,14 +159,14 @@
 
         def q_step(i, carry):
             wq_copy(layer, i).wait()
+            if layer == 0:
+                @pl.when(i < early)
+                def _():
+                    wo_copy(layer, i).start()
             qrow[:, pl.ds(pl.multiple_of(i * q_chunk, 128), q_chunk)] = dot(h8, wq[i])
             return carry
 
         lax.fori_loop(0, n_q, q_step, 0)
-        for copy in ffn_copies(layer):
-            copy.wait()
-        if layer == 0:
-            send_ffn(layer, True)
         pair = 2 * kv
         for j in range(heads_half // 2):
             block = qrow[:, j * pair:(j + 1) * pair]
@@ -194,6 +191,11 @@
             o = dot_nt(p, cbuf[layer, b, :latent, :])
             for h in range(heads_half):
                 lhs[b:b + 1, h * latent:(h + 1) * latent] = o[h:h + 1, :]
+            if layer == 0 and b and early + b - 1 < n_o:
+                wo_copy(layer, early + b - 1).start()
+                if b == 3:
+                    for copy in ffn_copies(layer):
+                        copy.start()
         lhs_b = lhs[...].astype(BF16)
 
         def o_step(i, carry):
@@ -206,6 +208,10 @@
 
         lax.fori_loop(0, n_o, o_step, 0)
         send(layer, 1, ysend.at[layer, 1], yrecv.at[layer], partner)
+        for copy in ffn_copies(layer):
+            copy.wait()
+        if layer == 0:
+            send_ffn(layer, True)
         if layer + 1 < layers:
             for b in range(2):
                 cache_copy(layer + 1, b).start()

time: 82.6 us -> 78 us (0.944)
  Pallas kernels: 81.9 us -> 77.3 us
    pallas_call x1, Pallas kernels: 81.9 us -> 77.3 us  [local_step(): pl.pallas_call(functools.partial(kernel, cfg), out_shape=pltpu.VMEM(x.sha...]
where the time goes in v5:
time: 78 us; the launch traced here: 77.9 us
  Pallas kernels  77.3 us (99%)
    pallas_call x1, Pallas kernels, local_step(): pl.pallas_call(functools.partial(kernel, cfg), out_shape=pltpu.VMEM(x.sha...  77.3 us

profile of v5, /device:TPU:0, one launch (start us, length us, event | category | flops | bytes accessed | tf_op | source)
XLA Modules:
  0.0 77.9 jit_solution(1582296999959655934)
XLA Ops:
  0.0 77.3 %mla_decode.1 = f32[2,2048]{1,0:T(2,128)S(1)} custom-call(bf16[2,2048]{1,0:T(2,128)(2,1)} %x_hbm.1, s32[2]{0:T(128)} %len_hbm.1, f32[2,2048]{1,0:T(2,128)} %ag_hbm.1, f32[2,2048]{1,0:T(2,128)} %fg_hbm.1, bf16[2,2,576,1024]{3,2,1,0:T(8,128)(2,1)} %bitcast.3, bf16[2,2048,9216]{2,1,0:T(8,128)(2,1)} %wq_hbm.1, bf16[2,8192,2048]{2,1,0:T(8,128)(2,1)} %wo_hbm.1, ...), custom_call_target="tpu_custom_call" | custom-call | tf_op jit(solution)/shard_map/mla_decode/pallas_call | solution.py:395
  77.3 0.6 convert_element_type.3

commit v6 on v4

--- a/solution.py
+++ b/solution.py
@@ -43,6 +43,7 @@
     n_q = qw // q_chunk
     n_o = d_model // o_chunk
     kdim = heads_half * latent
+    early = n_o - 3
     plane = side * side
     rows = 2 * side ** 3
     scale = (3 * (kv - latent)) ** -0.5
@@ -98,10 +99,6 @@
         wq_copy(0, i).start()
     for b in range(2):
         cache_copy(0, b).start()
-    for copy in ffn_copies(0):
-        copy.start()
-    for i in range(n_o):
-        wo_copy(0, i).start()
 
     barrier = pltpu.get_barrier_semaphore()
     peers = [partner] + [
@@ -151,12 +148,14 @@
 
         def q_step(i, carry):
             wq_copy(layer, i).wait()
+            if layer == 0:
+                @pl.when(i < early)
+                def _():
+                    wo_copy(layer, i).start()
             qrow[:, pl.ds(pl.multiple_of(i * q_chunk, 128), q_chunk)] = dot(h8, wq[i])
             return carry
 
         lax.fori_loop(0, n_q, q_step, 0)
-        for copy in ffn_copies(layer):
-            copy.wait()
         pair = 2 * kv
         for j in range(heads_half // 2):
             block = qrow[:, j * pair:(j + 1) * pair]
@@ -167,6 +166,8 @@
                     qbuf[layer, core, b, h:h + 1, :] = q8[b:b + 1, :]
                     qsend[layer, b, h:h + 1, :] = q8[2 + b:3 + b, :]
         send(layer, 2, qsend.at[layer], qbuf.at[layer, core], partner)
+        if layer == 0:
+            wo_copy(layer, early).start()
         positions = lax.broadcasted_iota(jnp.int32, (heads, seq), 1)
         for b in range(2):
             cache_copy(layer, b).wait()
@@ -180,6 +181,11 @@
             o = dot_nt(p, cbuf[layer, b, :latent, :])
             obuf[b, 0] = o[:heads_half]
             obuf[b, 1] = o[heads_half:]
+            if layer == 0:
+                wo_copy(layer, early + 1 + b).start()
+        if layer == 0:
+            for copy in ffn_copies(layer):
+                copy.start()
         for b in range(2):
             theirs = obuf[b, other]
             for h in range(heads_half):
@@ -203,6 +209,8 @@
 
         lax.fori_loop(0, n_o, o_step, 0)
         send(layer, 1, ysend.at[layer, 1], yrecv.at[layer], partner)
+        for copy in ffn_copies(layer):
+            copy.wait()
         if layer == 0:
             send_ffn(0, (2,))
         if layer + 1 < layers:

time: 83.7 us -> 79.9 us (0.955)
  Pallas kernels: 82.9 us -> 79.2 us
    pallas_call x1, Pallas kernels: 82.9 us -> 79.2 us  [local_step(): pl.pallas_call(functools.partial(kernel, cfg), out_shape=pltpu.VMEM(x.sha...]
where the time goes in v6:
time: 79.9 us; the launch traced here: 79.8 us
  Pallas kernels  79.2 us (99%)
    pallas_call x1, Pallas kernels, local_step(): pl.pallas_call(functools.partial(kernel, cfg), out_shape=pltpu.VMEM(x.sha...  79.2 us

profile of v6, /device:TPU:0, one launch (start us, length us, event | category | flops | bytes accessed | tf_op | source)
XLA Modules:
  0.0 79.8 jit_solution(17786593843456983553)
XLA Ops:
  0.0 79.2 %mla_decode.1 = f32[2,2048]{1,0:T(2,128)S(1)} custom-call(bf16[2,2048]{1,0:T(2,128)(2,1)} %x_hbm.1, s32[2]{0:T(128)} %len_hbm.1, f32[2,2048]{1,0:T(2,128)} %ag_hbm.1, f32[2,2048]{1,0:T(2,128)} %fg_hbm.1, bf16[2,2,576,1024]{3,2,1,0:T(8,128)(2,1)} %bitcast.3, bf16[2,2048,9216]{2,1,0:T(8,128)(2,1)} %wq_hbm.1, bf16[2,8192,2048]{2,1,0:T(8,128)(2,1)} %wo_hbm.1, ...), custom_call_target="tpu_custom_call" | custom-call | tf_op jit(solution)/shard_map/mla_decode/pallas_call | solution.py:398
  79.2 0.6 convert_element_type.3
